TPU v7x, 32 devices: a whole 2x2x4 slice. The times are simulated.
32 devices in a mesh: lon: 4 (over z), lat: 8 (over y, x, core).
Axes of the slice: x: 2, y: 2, z: 4, core: 2. Of those that a mesh axis runs over, the one named last changes fastest.
Arguments:
- travel_times: float32 [1024], P(('lon', 'lat')), may hold values from -6 to 6
- ray_counts: int32 [32], P(('lon', 'lat')), may hold values from 4 to 32
- tile_brick: int32 [1024, 4], P(('lon', 'lat')), may hold values from 0 to 31, all different within a row; in each aligned block of 32 rows (0 to 31, 32 to 63, ...) at most 8 rows name the same one
- cell_offsets: int32 [1024, 4, 128], P(('lon', 'lat')), may hold values from 0 to 1023
- cell_depths: int32 [1024, 4, 128], P(('lon', 'lat')), may hold values from 0 to 127
- seg_lengths: float32 [1024, 4, 128], P(('lon', 'lat')), may hold values from 0.002 to 0.02
Outputs:
- model: float32 [128, 256, 128], P('lon', 'lat')
- misfit: float32 [1024], P(('lon', 'lat'))
Inputs may be any that keep to these rules, and one draw needn't show every extreme that they name: `tile_brick`: among the 4 tiles of all rays of one device, no brick is named more than 8 times, a bound that some block reaches; a ray's tiles name different bricks; brick k lives on the device at position k of lon+lat. Only the first ray_counts rays of a device's 32 slots are live.
All inputs are finite; a program needn't handle non-finite values.
Results may differ from a plain program's by a relative error of at most 0.0014.
Values sent between devices are 32-bit elements; how exact they have to be, the bound alone decides.
No kernel may reach another device: no remote copies, remote signals or barrier semaphores. Data moves between devices by JAX's collectives and lax.ppermute only.
A program may use at most 64 MiB of HBM per device.

v0:
```python
import jax
import jax.numpy as jnp
from jax import lax
from jax.experimental import pallas as pl
from jax.experimental.pallas import tpu as pltpu
from jax.sharding import PartitionSpec as P

CLON = 32
CLAT = 32
DEP = 128
COLS = CLON * CLAT
ROWS_M = COLS // 2
ROWS_N = 2 * DEP
CH = 16
BLOCK = 16
WIN = 192

damping = 0.01
AXES = ("lon", "lat")
f32 = jnp.float32
i32 = jnp.int32
bf16 = jnp.bfloat16
SM = pl.BlockSpec(memory_space=pltpu.SMEM)
VM = pl.BlockSpec(memory_space=pltpu.VMEM)


def iota(shape, dim):
    return lax.broadcasted_iota(i32, shape, dim)


def sds(shape, dtype=f32):
    return jax.ShapeDtypeStruct(shape, dtype)


def call(kernel, outs, ins, args, scratch=(), out_specs=None, name=None):
    return pl.pallas_call(
        kernel,
        out_shape=outs,
        in_specs=list(ins),
        out_specs=out_specs if out_specs is not None else [VM] * len(outs),
        scratch_shapes=list(scratch),
        name=name,
    )(*args)


def lane_gather(x, index):
    return jnp.take_along_axis(x, index, axis=1, mode="promise_in_bounds")


def lane_order(m):
    lane = iota(m.shape, 1)
    key = m * 128 + lane
    size = 2
    while size <= 128:
        step = size // 2
        while step:
            other = lane_gather(key, lane ^ step)
            keep_low = ((lane & step) == 0) == ((lane & size) == 0)
            key = jnp.where(keep_low, jnp.minimum(key, other), jnp.maximum(key, other))
            step //= 2
        size *= 2
    return key & 127


def pack_kernel(devices, cap, rays, per_ray):
    width = 2 * cap + 1

    def kernel(brick, counts, times, offs, deps, lens, out, cells, lengths, used):
        lane = iota((1, 128), 1)
        out[...] = jnp.zeros_like(out)
        for i in range(0, offs.shape[0], 8):
            at = slice(i, i + 8)
            o = offs[at, :]
            m = o & (ROWS_M - 1)
            order = lane_order(m)
            key = (m * ROWS_N + (o >> 9) * DEP + deps[at, :]).astype(f32)
            cells[at, :] = lane_gather(key, order)
            lengths[at, :] = lane_gather(lens[at, :], order)

        def clear(d, carry):
            used[d] = 0
            return carry

        lax.fori_loop(0, devices, clear, 0)

        def one(r, row):
            value = times[r]
            for j in range(per_ray):
                b = brick[j, r]
                k = used[b]
                used[b] = k + 1
                base = b * width
                out[base + k] = cells[pl.ds(r * per_ray + j, 1), :]
                out[base + cap + k] = lengths[pl.ds(r * per_ray + j, 1), :]
                extra = out[base + 2 * cap]
                extra = jnp.where(lane == k, r.astype(f32), extra)
                out[base + 2 * cap] = jnp.where(lane == 16 + k, value, extra)
            return jnp.where(lane == 64 + r, value, row)

        row = lax.fori_loop(0, counts[0], one, jnp.zeros((1, 128), f32))

        def finish(d, carry):
            at = d * width + 2 * cap
            extra = jnp.where(lane >= 64, row, out[at])
            out[at] = jnp.where(lane == 127, used[d].astype(f32), extra)
            return carry

        lax.fori_loop(0, devices, finish, 0)

    return kernel


def split(x):
    high = x.astype(bf16).astype(f32)
    return high, x - high


def own_block():
    return (iota((8, 128), 1) >> (BLOCK.bit_length() - 1)) == iota((8, 128), 0)


def side_by_side(rows):
    mine = own_block()
    return jnp.concatenate(
        [colsum(jnp.where(mine, rows[8 * h : 8 * h + 8, :], 0.0)) for h in range(CH // 8)], axis=1
    )


GROUPS = 128 // BLOCK
LANES = CH * BLOCK
WINS = [128, 176] + [WIN] * (GROUPS - 4) + [176, 128]


def group_chunk(c, cell, w, gcell, gw, base, more):
    at = pl.multiple_of(c * CH, CH)
    turn = lambda ref: jnp.concatenate(
        [
            pltpu.roll(ref[pl.ds(at + 8 * h, 8), :], 0, 1, stride=BLOCK, stride_axis=0)
            for h in range(CH // 8)
        ],
        axis=0,
    )
    cells = turn(cell)
    lens = turn(w)
    rest = jnp.int32(0)
    for j in range(GROUPS):
        shift = (128 - j * BLOCK) % 128
        gc = side_by_side(pltpu.roll(cells, shift, 1) if j else cells)
        gl = side_by_side(pltpu.roll(lens, shift, 1) if j else lens)
        gcell[pl.ds(c * GROUPS + j, 1), :] = gc
        gw[pl.ds(c * GROUPS + j, 1), :] = gl
        m = gc.astype(i32) >> 8
        low = jnp.min(jnp.where(gl != 0.0, m, ROWS_M - 1))
        high = jnp.max(jnp.where(gl != 0.0, m, 0))
        first = jnp.minimum((low >> 4) << 4, ROWS_M - WINS[j])
        base[c * GROUPS + j] = first
        rest = jnp.maximum(rest, high - first + 1 - WINS[j])
    more[c] = (rest + WIN - 1) // WIN


def main_window(c, j, base, m):
    at = pl.multiple_of(base[c * GROUPS + j], 16)
    return at, m - at, WINS[j]


def more_window(c, i, base, m):
    j = i % GROUPS
    start = base[c * GROUPS + j] + (i // GROUPS) * WIN
    for k, rows in enumerate(WINS):
        start = start + jnp.where(j == k, rows, 0)
    at = pl.multiple_of(jnp.minimum(start, ROWS_M - WIN), 16)
    return at, jnp.where(m >= start, m - at, -1), WIN


def down(row, rows):
    tile = jnp.broadcast_to(row.astype(f32), (16, row.shape[1])).astype(bf16)
    return jnp.concatenate([tile] * (rows // 16), axis=0)


def row_ids(rows):
    return iota((rows, LANES), 0).astype(f32).astype(bf16)


def chunks_of(total):
    return (total + CH - 1) // CH


def scatter_tiles(total, gcell, gw, base, more, b_ref, acc, ahead=None):
    acc[...] = jnp.zeros_like(acc)
    ids = row_ids(ROWS_N)
    one = jnp.ones((), bf16)
    zero = jnp.zeros((), bf16)
    dims = (((1,), (1,)), ((), ()))

    def group(c, j, window, b):
        g = c * GROUPS + j % GROUPS
        ci = gcell[pl.ds(g, 1), :].astype(i32)
        at, m, rows = window(c, j, base, ci >> 8)
        high, low = split(gw[pl.ds(g, 1), :] * b)
        ohm = jnp.where(ids[:rows] == down(m, rows), one, zero)
        hit = ids == down(ci & (ROWS_N - 1), ROWS_N)
        vh = jnp.where(hit, down(high, ROWS_N), zero)
        vl = jnp.where(hit, down(low, ROWS_N), zero)
        acc[pl.ds(at, rows), :] += lax.dot_general(
            ohm, vh, dims, preferred_element_type=f32
        ) + lax.dot_general(ohm, vl, dims, preferred_element_type=f32)

    def chunk(c, carry):
        at = pl.multiple_of(c * CH, CH)
        b = side_by_side(b_ref[pl.ds(at, CH), :])
        for j in range(GROUPS):
            group(c, j, main_window, b)
        if ahead is not None:
            ahead(c + 1)

        @pl.when(more[c] > 0)
        def _():
            def again(i, carry):
                group(c, i, more_window, b)
                return carry

            lax.fori_loop(0, more[c] * GROUPS, again, 0)

        return carry

    if ahead is not None:
        ahead(0)
    lax.fori_loop(0, chunks_of(total), chunk, 0)


def gather_tiles(total, gcell, gw, base, more, gh, gl, got, yv):
    yv[...] = jnp.zeros_like(yv)
    ids = row_ids(ROWS_N)
    one = jnp.ones((), bf16)
    zero = jnp.zeros((), bf16)

    def group(c, j, window):
        g = c * GROUPS + j % GROUPS
        ci = gcell[pl.ds(g, 1), :].astype(i32)
        at, m, rows = window(c, j, base, ci >> 8)
        ohn = jnp.where(ids == down(ci & (ROWS_N - 1), ROWS_N), one, zero)
        full = jnp.dot(gh[pl.ds(at, rows), :], ohn, preferred_element_type=f32) + jnp.dot(
            gl[pl.ds(at, rows), :], ohn, preferred_element_type=f32
        )
        return colsum(jnp.where(iota((rows, LANES), 0) == m, full, 0.0)) * gw[pl.ds(g, 1), :]

    def chunk(c, carry):
        part = group(c, 0, main_window)
        for j in range(1, GROUPS):
            part = part + group(c, j, main_window)
        got[...] = part

        @pl.when(more[c] > 0)
        def _():
            def again(i, carry):
                got[...] += group(c, i, more_window)
                return carry

            lax.fori_loop(0, more[c] * GROUPS, again, 0)

        mine = own_block()
        for h in range(CH // 8):
            at = pl.multiple_of(c * CH + 8 * h, 8)
            yv[pl.ds(at, 8), :] = jnp.where(mine, got[:, 128 * h : 128 * (h + 1)], 0.0)
        return carry

    lax.fori_loop(0, chunks_of(total), chunk, 0)


def lat_rows(src, at):
    return src[pl.ds(at, CLON, stride=CLAT), :]


def layers(src, lo, hi, la, lb):
    lo[...] = src[0:CLAT, :]
    hi[...] = src[COLS - CLAT : COLS, :]
    la[...] = lat_rows(src, 0)
    lb[...] = lat_rows(src, CLAT - 1)


LAYERS = [(CLAT, DEP), (CLAT, DEP), (CLON, DEP), (CLON, DEP)]


def depth_part(c):
    lane = iota(c.shape, 1)
    dm = jnp.where(lane == 0, 0.0, pltpu.roll(c, 1, 1))
    dp = jnp.where(lane == DEP - 1, 0.0, pltpu.roll(c, DEP - 1, 1))
    return 6.0 * c - dm - dp


def stencil_rows(c, up, down, lat_before, lat_after):
    sub = iota(c.shape, 0)
    lm = jnp.where(sub == 0, lat_before, pltpu.roll(c, 1, 0))
    lp = jnp.where(sub == CLAT - 1, lat_after, pltpu.roll(c, CLAT - 1, 0))
    return depth_part(c) - up - down - lm - lp


def stencil_layer(i, src, before, after, lat_before, lat_after):
    c = src[i * CLAT : (i + 1) * CLAT, :]
    up = before[...] if i == 0 else src[(i - 1) * CLAT : i * CLAT, :]
    down = after[...] if i == CLON - 1 else src[(i + 1) * CLAT : (i + 2) * CLAT, :]
    return stencil_rows(c, up, down, lat_before[i : i + 1, :], lat_after[i : i + 1, :])


def colsum(x):
    return jnp.sum(x, axis=0, keepdims=True)


def start_kernel(devices, cap, rays):
    width = 2 * cap + 1

    def kernel(
        recv, g, lo, hi, gcell, gw, q, data, total, base, more, cell, w, b, acc
    ):
        sub = iota((cap, 128), 0)
        lane = iota((cap, 128), 1)
        lane1 = iota((1, 128), 1)
        q[...] = jnp.full_like(q, -1.0)
        per_row = 128 // rays
        pos = 0
        row = jnp.zeros((1, 128), f32)
        for s in range(devices):
            at = s * width
            ext = recv[at + 2 * cap]
            wide = jnp.broadcast_to(ext, (cap, 128))
            qs = jnp.sum(jnp.where(lane == sub, wide, 0.0), axis=1, keepdims=True)
            bs = jnp.sum(jnp.where(lane == sub + 16, wide, 0.0), axis=1, keepdims=True)
            cell[pl.ds(pos, cap), :] = jnp.concatenate([recv[at + k] for k in range(cap)], axis=0)
            w[pl.ds(pos, cap), :] = jnp.concatenate(
                [recv[at + cap + k] for k in range(cap)], axis=0
            )
            q[pl.ds(pos, cap), :] = jnp.broadcast_to(qs + float(s * rays), (cap, 128))
            b[pl.ds(pos, cap), :] = jnp.broadcast_to(bs, (cap, 128))
            pos = pos + jnp.max(jnp.where(lane1 == 127, ext, 0.0).astype(i32))
            j = s % per_row
            moved = pltpu.roll(ext, (j * rays - 64) % 128, 1)
            inside = (lane1 >= j * rays) & (lane1 < (j + 1) * rays)
            row = jnp.where(inside, moved, row)
            if j == per_row - 1:
                data[s // per_row : s // per_row + 1, :] = row
        w[pl.ds(pos, CH), :] = jnp.zeros((CH, 128), f32)
        b[pl.ds(pos, CH), :] = jnp.zeros((CH, 128), f32)
        q[pl.ds(pos, CH), :] = jnp.full((CH, 128), -1.0, f32)
        total[0] = pos
        ahead = lambda c: group_chunk(c, cell, w, gcell, gw, base, more)
        scatter_tiles(pos, gcell, gw, base, more, b, acc, ahead)
        g[0:ROWS_M, :] = acc[:, :DEP]
        g[ROWS_M:COLS, :] = acc[:, DEP:]
        lo[...] = g[: 2 * CLAT, :]
        hi[...] = g[COLS - 2 * CLAT :, :]

    return kernel


def ray_places(q):
    qi = q[...].astype(i32)
    return qi >> 7, (qi & 127) == iota(qi.shape, 1)


def forward_kernel(ray_rows):
    def kernel(total, base, more, src, gcell, gw, q, y, gh, gl, got, yv):
        for half in range(2):
            rows = slice(half * ROWS_M, (half + 1) * ROWS_M)
            cols = slice(half * DEP, (half + 1) * DEP)
            high, low = split(src[rows, :])
            gh[:, cols] = high.astype(bf16)
            gl[:, cols] = low.astype(bf16)
        gather_tiles(total[0], gcell, gw, base, more, gh, gl, got, yv)
        high, here = ray_places(q)
        ys = jnp.where(here, jnp.sum(yv[...], axis=1, keepdims=True), 0.0)
        for i in range(ray_rows):
            y[i : i + 1, :] = colsum(jnp.where(high == i, ys, 0.0))

    return kernel


def send_copies(out, devices, rows):
    count = len(rows)

    def one(d, carry):
        for i, row in enumerate(rows):
            out[d * count + i] = row
        return carry

    lax.fori_loop(0, devices, one, 0)


SIDE = (2, CLON + 2, DEP)


def edge_kernel(devices, ray_rows):
    def kernel(g, before, after, y, la, lb, out):
        for out_ref, lats in ((la, (0, 1)), (lb, (CLAT - 1, CLAT - 2))):
            for k, at in enumerate(lats):
                out_ref[k, 1 : CLON + 1, :] = lat_rows(g, at)
                out_ref[k, 0:1, :] = before[CLAT + at : CLAT + at + 1, :]
                out_ref[k, CLON + 1 : CLON + 2, :] = after[at : at + 1, :]
        gg = jnp.zeros((CLAT, DEP), f32)
        for i in range(CLON):
            c = g[i * CLAT : (i + 1) * CLAT, :]
            gg = gg + c * c
        send_copies(out, devices, [y[i : i + 1, :] for i in range(ray_rows)] + [colsum(gg)])

    return kernel


def received(recv, devices, count):
    def one(d, acc):
        return acc + recv[pl.ds(d * count, count)]

    return lax.fori_loop(0, devices, one, jnp.zeros((count, 1, 128), f32))


def all_rows(acc, start, count):
    return jnp.concatenate([acc[start + i] for i in range(count)], axis=0)


def total_of(x):
    return jnp.sum(jnp.sum(x, axis=0, keepdims=True), axis=1, keepdims=True)


def in_lanes(numbers):
    lane = iota((1, 128), 1)
    packed = jnp.zeros((1, 128), f32)
    for i, x in enumerate(numbers):
        packed = jnp.where(lane == i, x, packed)
    return packed


def second_kernel(devices, ray_rows):
    def kernel(
        total, base, more, place, recv, data_ref, g, before, after, side_before, side_after, gcell, gw, q,
        z, lo, hi, la, lb, q1, p1_ref, r2_ref, num, b, acc, qb, qa, qlb, qla,
    ):
        data = data_ref[...]
        got = received(recv, devices, ray_rows + 1)
        p1 = all_rows(got, 0, ray_rows)
        gg = total_of(got[ray_rows])
        beta1 = jnp.sqrt(total_of(data * data))
        nrm = jnp.sqrt(gg)
        alpha1 = nrm / beta1
        r2 = p1 / nrm - alpha1 * (data / beta1)
        p1_ref[...] = p1
        r2_ref[...] = r2
        num[...] = in_lanes([nrm, beta1, alpha1, total_of(r2 * r2), gg])
        high, here = ray_places(q)
        picked = jnp.zeros(q.shape, f32)
        for i in range(ray_rows):
            picked = jnp.where(high == i, r2[i : i + 1, :], picked)
        picked = jnp.sum(jnp.where(here, picked, 0.0), axis=1, keepdims=True)
        b[...] = jnp.broadcast_to(picked, b.shape)
        scatter_tiles(total[0], gcell, gw, base, more, b, acc)

        near_b = side_before[0, 1 : CLON + 1, :]
        near_a = side_after[0, 1 : CLON + 1, :]
        for out_ref, near, far, side, edge in (
            (qlb, near_b, side_before, 0, 0),
            (qla, near_a, side_after, CLAT - 1, 1),
        ):
            res = depth_part(near) - far[0, 0:CLON, :] - far[0, 2 : CLON + 2, :]
            res = res - far[1, 1 : CLON + 1, :] - lat_rows(g, side)
            out_ref[...] = jnp.where(place[edge] == 0, 0.0, res)
        qb[...] = stencil_rows(
            before[CLAT:, :], before[:CLAT, :], g[:CLAT, :], side_before[0, 0:1, :], side_after[0, 0:1, :]
        )
        qa[...] = stencil_rows(
            after[:CLAT, :], g[COLS - CLAT :, :], after[CLAT:, :],
            side_before[0, CLON + 1 :, :], side_after[0, CLON + 1 :, :],
        )
        for i in range(CLON):
            c = g[i * CLAT : (i + 1) * CLAT, :]
            up = before[CLAT:, :] if i == 0 else g[(i - 1) * CLAT : i * CLAT, :]
            down = after[:CLAT, :] if i == CLON - 1 else g[(i + 1) * CLAT : (i + 2) * CLAT, :]
            q1[i * CLAT : (i + 1) * CLAT, :] = stencil_rows(
                c, up, down, near_b[i : i + 1, :], near_a[i : i + 1, :]
            )
        scale = (damping * damping) / nrm
        for i in range(CLON):
            half, at = divmod(i * CLAT, ROWS_M)
            h = acc[at : at + CLAT, half * DEP : (half + 1) * DEP]
            z[i * CLAT : (i + 1) * CLAT, :] = h + scale * stencil_layer(i, q1, qb, qa, qlb, qla)
        layers(z, lo, hi, la, lb)

    return kernel


def last_smooth_kernel(devices, ray_rows):
    def kernel(z, g, q1, before, after, lat_before, lat_after, y, out):
        sums = [jnp.zeros((CLAT, DEP), f32) for _ in range(5)]
        for i in range(CLON):
            res = stencil_layer(i, z, before, after, lat_before, lat_after)
            rows = slice(i * CLAT, (i + 1) * CLAT)
            c, q, first = z[rows, :], q1[rows, :], g[rows, :]
            terms = [c * c, c * first, res * res, res * q, q * q]
            sums = [x + t for x, t in zip(sums, terms)]
        row = in_lanes([total_of(x) for x in sums])
        send_copies(out, devices, [y[i : i + 1, :] for i in range(ray_rows)] + [row])

    return kernel


def final_kernel(devices, ray_rows, rays):
    def kernel(me, recv, data, p1, r2, num, g, z, model, misfit):
        got = received(recv, devices, ray_rows + 1)
        p2 = all_rows(got, 0, ray_rows)
        nums = got[ray_rows]
        zz, zg, ll, lq, qq = [nums[0:1, i : i + 1] for i in range(5)]
        nrm, beta1, alpha1, rr, gg = [num[0:1, i : i + 1] for i in range(5)]
        beta2 = jnp.sqrt(rr + (damping * damping) * (qq / gg))
        kappa = (beta2 * beta2) / nrm
        size = jnp.sqrt(zz - 2.0 * kappa * zg + kappa * kappa * gg)
        lw = ll - 2.0 * kappa * lq + kappa * kappa * qq
        lwq = lq - kappa * qq
        alpha2 = size / beta2
        av1 = p1[...] / nrm
        av2 = (p2 - kappa * p1[...]) / size
        r3 = av2 - alpha2 * (r2[...] / beta2)
        x = alpha2 / (nrm * beta2)
        grid = (lw / size - 2.0 * x * lwq) / size + (x * x) * qq
        beta3sq = total_of(r3 * r3) + (damping * damping) * grid
        rho = jnp.sqrt(alpha1 * alpha1 + beta2 * beta2)
        cosine = alpha1 / rho
        sine = beta2 / rho
        theta = sine * alpha2
        rho_bar = -cosine * alpha2
        k1 = cosine * beta1 / rho
        t = theta / rho
        phi_bar = sine * beta1
        rho2 = jnp.sqrt(rho_bar * rho_bar + beta3sq)
        k2 = (rho_bar / rho2) * phi_bar / rho2
        first = k1 - k2 * t
        second = k2 / size
        model[...] = (first / nrm - second * kappa) * g[...] + second * z[...]
        mis = data[...] - (first * av1 + k2 * av2)
        per_row = 128 // rays
        d = me[0]
        sub = iota(mis.shape, 0)
        mine = colsum(jnp.where(sub == d // per_row, mis, 0.0))
        misfit[...] = pltpu.roll(mine, (128 - (d % per_row) * rays) % 128, 1)

    return kernel


def exchange_all(x):
    return lax.all_to_all(x, AXES, split_axis=0, concat_axis=0, tiled=True)


def ring(axis, wrap):
    n = lax.axis_size(axis)
    up = [(i, (i + 1) % n) for i in range(n if wrap else n - 1)]
    return up, [(j, i) for i, j in up]


def lon_halo(lo, hi):
    up, down = ring("lon", True)
    return lax.ppermute(hi, "lon", up), lax.ppermute(lo, "lon", down)


def lat_halo(la, lb):
    up, down = ring("lat", False)
    return lax.ppermute(lb, "lat", up), lax.ppermute(la, "lat", down)


def shards(travel_times, ray_counts, tile_brick, cell_offsets, cell_depths, seg_lengths):
    devices = lax.axis_size(AXES)
    rays, per_ray, segs = cell_offsets.shape
    tiles = rays * per_ray
    slots = 2 * tiles
    cap = slots // devices
    width = 2 * cap + 1
    ray_rows = devices * rays // 128
    room = slots + CH
    flat = lambda x: x.reshape(tiles, segs)
    layer_outs = [sds(s) for s in LAYERS]
    grid = sds((COLS, DEP))
    buf = lambda dtype: pltpu.VMEM((ROWS_M, ROWS_N), dtype)

    (packed,) = call(
        pack_kernel(devices, cap, rays, per_ray),
        [sds((devices * width, 1, 128))],
        [SM, SM, SM, VM, VM, VM],
        (tile_brick.T, ray_counts, travel_times, flat(cell_offsets), flat(cell_depths), flat(seg_lengths)),
        [pltpu.VMEM((tiles, segs), f32)] * 2 + [pltpu.SMEM((devices,), i32)],
        name="pack",
    )
    recv0 = exchange_all(packed)
    chunks = room // CH + 1
    grouped = sds((chunks * GROUPS, LANES))
    g, lo, hi, gcell, gw, q, data, total, base, more = call(
        start_kernel(devices, cap, rays),
        [grid, sds((2 * CLAT, DEP)), sds((2 * CLAT, DEP)), grouped, grouped, sds((room, 128)), sds((ray_rows, 128)),
         sds((1,), i32), sds((chunks * GROUPS,), i32), sds((chunks,), i32)],
        [VM],
        (recv0,),
        [pltpu.VMEM((room + CH, 128), f32)] * 2 + [pltpu.VMEM((room, 128), f32), buf(f32)],
        out_specs=[VM] * 7 + [SM] * 3,
        name="start",
    )
    gather_scratch = [buf(bf16), buf(bf16), pltpu.VMEM((1, LANES), f32), pltpu.VMEM((room, 128), f32)]
    tiles_of = (total, base, more)
    before, after = lon_halo(lo, hi)
    (y1,) = call(
        forward_kernel(ray_rows), [sds((ray_rows, 128))], [SM] * 3 + [VM] * 4, (*tiles_of, g, gcell, gw, q),
        gather_scratch, name="forward",
    )
    la, lb, send = call(
        edge_kernel(devices, ray_rows),
        [sds(SIDE), sds(SIDE), sds((devices * (ray_rows + 1), 1, 128))],
        [VM] * 4,
        (g, before, after, y1),
        name="edge",
    )
    sides = lat_halo(la, lb)
    recv1 = exchange_all(send)
    lat = lax.axis_index("lat")
    place = jnp.stack([lat, lax.axis_size("lat") - 1 - lat]).astype(i32)
    z, lo, hi, la, lb, q1, p1, r2, num = call(
        second_kernel(devices, ray_rows),
        [grid, *layer_outs, grid, sds((ray_rows, 128)), sds((ray_rows, 128)), sds((1, 128))],
        [SM] * 4 + [VM] * 10,
        (*tiles_of, place, recv1, data, g, before, after, *sides, gcell, gw, q),
        [pltpu.VMEM((room, 128), f32), buf(f32)] + [pltpu.VMEM((CLAT, DEP), f32)] * 4,
        name="second",
    )
    around = lon_halo(lo, hi) + lat_halo(la, lb)
    (y2,) = call(
        forward_kernel(ray_rows), [sds((ray_rows, 128))], [SM] * 3 + [VM] * 4, (*tiles_of, z, gcell, gw, q),
        gather_scratch, name="forward",
    )
    (send,) = call(
        last_smooth_kernel(devices, ray_rows),
        [sds((devices * (ray_rows + 1), 1, 128))],
        [VM] * 8,
        (z, g, q1, *around, y2),
        name="last_smooth",
    )
    recv2 = exchange_all(send)
    me = lax.axis_index(AXES).astype(i32).reshape(1)
    model, mis = call(
        final_kernel(devices, ray_rows, rays),
        [grid, sds((1, 128))],
        [SM] + [VM] * 7,
        (me, recv2, data, p1, r2, num, g, z),
        name="final",
    )
    return model.reshape(CLON, CLAT, DEP), mis[0, :rays]


def solution(mesh):
    placed = (
        P(("lon", "lat")),
        P(("lon", "lat")),
        P(("lon", "lat"), None),
        P(("lon", "lat"), None, None),
        P(("lon", "lat"), None, None),
        P(("lon", "lat"), None, None),
    )
    return jax.shard_map(
        shards,
        mesh=mesh,
        in_specs=placed,
        out_specs=(P("lon", "lat", None), P(("lon", "lat"))),
        check_vma=False,
    )
```

profile of v0, /device:TPU:0, one launch (start us, length us, event | category | flops | bytes accessed | tf_op | source)
XLA Modules:
  0.0 112.0 jit_solution(5691166187323013560)
XLA Ops:
  1.3 5.0 %pack.1 = f32[544,1,128]{2,1,0:T(1,128)} custom-call(s32[4,32]{1,0:T(4,128)} %bitcast.13, s32[1]{0:T(128)S(6)} %copy.8.counts, f32[32]{0:T(128)} %times.1, s32[128,128]{1,0:T(8,128)} %bitcast.10, s32[128,128]{1,0:T(8,128)} %bitcast.11, f32[128,128]{1,0:T(8,128)} %bitcast.12), custom_call_target="tpu_custom_call" | custom-call | tf_op jit(solution)/shard_map/pack/pallas_call | solution.py:36
  6.3 18.2 %all_to_all.15.recv = f32[544,1,128]{2,1,0:T(1,128)} all-to-all(f32[544,1,128]{2,1,0:T(1,128)} %pack.1), channel_id=1, replica_groups=mesh['lon'=4,'lat'=8] {'lon','lat'}, dimensions={0} | all-to-all | bytes 557056 | tf_op jit(solution)/shard_map/all_to_all | solution.py:545
  24.5 6.1 %start.1 = (f32[1024,128]{1,0:T(8,128)}, f32[64,128]{1,0:T(8,128)}, f32[64,128]{1,0:T(8,128)}, f32[144,256]{1,0:T(8,128)}, f32[144,256]{1,0:T(8,128)}, /*index=5...) custom-call(f32[544,1,128]{2,1,0:T(1,128)} %all_to_all.15.recv), custom_call_target="tpu_custom_call" | custom-call | tf_op jit(solution)/shard_map/start/pallas_call | solution.py:36
  30.6 1.7 %collective-permute-start = (f32[64,128]{1,0:T(8,128)}, f32[64,128]{1,0:T(8,128)S(1)}, u32[]{:S(2)}, u32[]{:S(2)}) collective-permute-start(f32[64,128]{1,0:T(8,128)} %get-tuple-element.30), channel_id=1, source_target_pairs={{0,8},{8,16},{16,24},{24,0},{1,9},{9,17},{17,25},{25,1},{2,10},{10... | collective-permute-start | bytes 98312 | tf_op jit(solution)/shard_map/ppermute | solution.py:556
  32.3 2.2 %collective-permute-start.1 = (f32[64,128]{1,0:T(8,128)}, f32[64,128]{1,0:T(8,128)S(1)}, u32[]{:S(2)}, u32[]{:S(2)}) collective-permute-start(f32[64,128]{1,0:T(8,128)} %get-tuple-element.31), channel_id=1, source_target_pairs={{8,0},{16,8},{24,16},{0,24},{9,1},{17,9},{25,17},{1,25},{10,2},{18... | collective-permute-start | bytes 98312 | tf_op jit(solution)/shard_map/ppermute | solution.py:556
  34.5 4.4 %forward.2.y = f32[8,128]{1,0:T(8,128)} custom-call(s32[1]{0:T(128)} %get-tuple-element.26.total, s32[144]{0:T(256)} %get-tuple-element.27.base, s32[18]{0:T(128)} %get-tuple-element.28.more, f32[1024,128]{1,0:T(8,128)} %get-tuple-element.29.src.g, f32[144,256]{1,0:T(8,128)} %get-tuple-element.32.gcell, f32[144,256]{1,0:T(8,128)} %get-tuple-element.33.gw, ...), custom_call_target="tpu_custom_call" | custom-call | tf_op jit(solution)/shard_map/forward/pallas_call | solution.py:36
  38.9 0.6 copy-done.2
  39.5 0.6 copy-done.3
  40.1 2.0 %edge.1 = (f32[2,34,128]{2,1,0:T(8,128)}, f32[2,34,128]{2,1,0:T(8,128)}, f32[288,1,128]{2,1,0:T(1,128)}) custom-call(f32[1024,128]{1,0:T(8,128)} %get-tuple-element.29.src.g, f32[64,128]{1,0:T(8,128)} %copy-done.2, f32[64,128]{1,0:T(8,128)} %copy-done.3, f32[8,128]{1,0:T(8,128)} %forward.2.y), custom_call_target="tpu_custom_call" | custom-call | tf_op jit(solution)/shard_map/edge/pallas_call | solution.py:36
  42.1 10.7 %all-to-all-start.1 = ((f32[288,1,128]{2,1,0:T(1,128)}), f32[288,1,128]{2,1,0:T(1,128)S(1)}, u32[]{:S(2)}, u32[]{:S(2)}) async-start(f32[288,1,128]{2,1,0:T(1,128)} %get-tuple-element.35), calls=%async_computation.1 | async-start | bytes 294912 | tf_op jit(solution)/shard_map/all_to_all | solution.py:545
  52.9 2.2 %collective-permute-start.2 = (f32[2,34,128]{2,1,0:T(8,128)S(1)}, f32[2,34,128]{2,1,0:T(8,128)S(1)}, u32[]{:S(2)}, u32[]{:S(2)}) collective-permute-start(f32[2,34,128]{2,1,0:T(8,128)S(1)} %copy-done.11), channel_id=1, source_target_pairs={{0,1},{1,2},{2,3},{3,4},{4,5},{5,6},{6,7},{8,9},{9,10},{10,11},{11... | collective-permute-start | bytes 104456 | tf_op jit(solution)/shard_map/ppermute | solution.py:561
  55.0 1.3 %collective-permute-start.3 = (f32[2,34,128]{2,1,0:T(8,128)S(1)}, f32[2,34,128]{2,1,0:T(8,128)S(1)}, u32[]{:S(2)}, u32[]{:S(2)}) collective-permute-start(f32[2,34,128]{2,1,0:T(8,128)S(1)} %copy-done.10), channel_id=1, source_target_pairs={{1,0},{2,1},{3,2},{4,3},{5,4},{6,5},{7,6},{9,8},{10,9},{11,10},{12... | collective-permute-start | bytes 104456 | tf_op jit(solution)/shard_map/ppermute | solution.py:561
  56.3 0.7 pad_add_fusion.place
  57.0 2.3 %collective-permute-done.3.side_after = f32[2,34,128]{2,1,0:T(8,128)S(1)} collective-permute-done((f32[2,34,128]{2,1,0:T(8,128)S(1)}, f32[2,34,128]{2,1,0:T(8,128)S(1)}, u32[]{:S(2)}, u32[]{:S(2)}) %collective-permute-start.3) | collective-permute-done | bytes 34848 | tf_op jit(solution)/shard_map/ppermute | solution.py:561
  59.3 2.0 %all-to-all-done.1.recv = f32[288,1,128]{2,1,0:T(1,128)S(1)} async-done(((f32[288,1,128]{2,1,0:T(1,128)}), f32[288,1,128]{2,1,0:T(1,128)S(1)}, u32[]{:S(2)}, u32[]{:S(2)}) %all-to-all-start.1) | async-done | bytes 147488 | tf_op jit(solution)/shard_map/all_to_all | solution.py:545
  61.3 0.6 copy-done
  61.9 6.7 %second.1 = (f32[1024,128]{1,0:T(8,128)}, f32[32,128]{1,0:T(8,128)}, f32[32,128]{1,0:T(8,128)}, f32[32,128]{1,0:T(8,128)}, f32[32,128]{1,0:T(8,128)}, /*index=5*...) custom-call(s32[1]{0:T(128)} %get-tuple-element.26.total, s32[144]{0:T(256)} %get-tuple-element.27.base, ...), custom_call_target="tpu_custom_call" | custom-call | tf_op jit(solution)/shard_map/second/pallas_call | solution.py:36
  68.6 1.6 %collective-permute-start.4 = (f32[32,128]{1,0:T(8,128)}, f32[32,128]{1,0:T(8,128)S(1)}, u32[]{:S(2)}, u32[]{:S(2)}) collective-permute-start(f32[32,128]{1,0:T(8,128)} %get-tuple-element.41), channel_id=1, source_target_pairs={{0,8},{8,16},{16,24},{24,0},{1,9},{9,17},{17,25},{25,1},{2,10},{10... | collective-permute-start | bytes 49160 | tf_op jit(solution)/shard_map/ppermute | solution.py:556
  70.2 2.3 %collective-permute-start.5 = (f32[32,128]{1,0:T(8,128)}, f32[32,128]{1,0:T(8,128)S(1)}, u32[]{:S(2)}, u32[]{:S(2)}) collective-permute-start(f32[32,128]{1,0:T(8,128)} %get-tuple-element.42), channel_id=1, source_target_pairs={{8,0},{16,8},{24,16},{0,24},{9,1},{17,9},{25,17},{1,25},{10,2},{18... | collective-permute-start | bytes 49160 | tf_op jit(solution)/shard_map/ppermute | solution.py:556
  72.5 4.6 %collective-permute-start.6 = (f32[32,128]{1,0:T(8,128)}, f32[32,128]{1,0:T(8,128)S(1)}, u32[]{:S(2)}, u32[]{:S(2)}) collective-permute-start(f32[32,128]{1,0:T(8,128)} %get-tuple-element.43), channel_id=1, source_target_pairs={{0,1},{1,2},{2,3},{3,4},{4,5},{5,6},{6,7},{8,9},{9,10},{10,11},{11... | collective-permute-start | bytes 49160 | tf_op jit(solution)/shard_map/ppermute | solution.py:561
  77.1 1.3 %collective-permute-start.7 = (f32[32,128]{1,0:T(8,128)}, f32[32,128]{1,0:T(8,128)S(1)}, u32[]{:S(2)}, u32[]{:S(2)}) collective-permute-start(f32[32,128]{1,0:T(8,128)} %get-tuple-element.44), channel_id=1, source_target_pairs={{1,0},{2,1},{3,2},{4,3},{5,4},{6,5},{7,6},{9,8},{10,9},{11,10},{12... | collective-permute-start | bytes 49160 | tf_op jit(solution)/shard_map/ppermute | solution.py:561
  78.4 4.4 %forward.3.y = f32[8,128]{1,0:T(8,128)} custom-call(s32[1]{0:T(128)} %get-tuple-element.26.total, s32[144]{0:T(256)} %get-tuple-element.27.base, s32[18]{0:T(128)} %get-tuple-element.28.more, f32[1024,128]{1,0:T(8,128)} %get-tuple-element.39.src.z, f32[144,256]{1,0:T(8,128)} %get-tuple-element.32.gcell, f32[144,256]{1,0:T(8,128)} %get-tuple-element.33.gw, ...), custom_call_target="tpu_custom_call" | custom-call | tf_op jit(solution)/shard_map/forward/pallas_call | solution.py:36
  82.9 0.5 copy-done.6
  83.4 0.0 copy-done.8
  83.4 0.0 copy-done.9
  83.5 2.7 %last_smooth.1 = f32[288,1,128]{2,1,0:T(1,128)} custom-call(f32[1024,128]{1,0:T(8,128)} %get-tuple-element.39.src.z, f32[1024,128]{1,0:T(8,128)} %get-tuple-element.29.src.g, f32[1024,128]{1,0:T(8,128)} %get-tuple-element.40.q1, f32[32,128]{1,0:T(8,128)} %copy-done.6, f32[32,128]{1,0:T(8,128)} %copy-done.7, f32[32,128]{1,0:T(8,128)} %copy-done.8, ...), custom_call_target="tpu_custom_call" | custom-call | tf_op jit(solution)/shard_map/last_smooth/pallas_call | solution.py:36
  86.2 12.8 %all-to-all-start.2 = ((f32[288,1,128]{2,1,0:T(1,128)}), f32[288,1,128]{2,1,0:T(1,128)S(1)}, u32[]{:S(2)}, u32[]{:S(2)}) async-start(f32[288,1,128]{2,1,0:T(1,128)} %last_smooth.1), calls=%async_computation.2 | async-start | bytes 294912 | tf_op jit(solution)/shard_map/all_to_all | solution.py:545
  99.0 8.4 %all-to-all-done.2.recv = f32[288,1,128]{2,1,0:T(1,128)S(1)} async-done(((f32[288,1,128]{2,1,0:T(1,128)}), f32[288,1,128]{2,1,0:T(1,128)S(1)}, u32[]{:S(2)}, u32[]{:S(2)}) %all-to-all-start.2) | async-done | bytes 147488 | tf_op jit(solution)/shard_map/all_to_all | solution.py:545
  107.4 0.6 copy-done.1
  108.0 2.8 %final.1 = (f32[1024,128]{1,0:T(8,128)}, f32[1,128]{1,0:T(1,128)}) custom-call(s32[1]{0:T(128)} %bitcast.me, f32[288,1,128]{2,1,0:T(1,128)} %copy-done.1, f32[8,128]{1,0:T(8,128)} %get-tuple-element.36.data_ref.data, f32[8,128]{1,0:T(8,128)} %get-tuple-element.45.p1, f32[8,128]{1,0:T(8,128)} %get-tuple-element.46.r2, f32[1,128]{1,0:T(1,128)} %get-tuple-element.47.num, ...), custom_call_target="tpu_custom_call" | custom-call | tf_op jit(solution)/shard_map/final/pallas_call | solution.py:36
  110.8 0.7 copy-done.12
  111.5 0.5 slice_bitcast_fusion
  (25 shorter events, 0.1 us)
Async XLA Ops:
  30.6 8.3 %collective-permute-start = (f32[64,128]{1,0:T(8,128)}, f32[64,128]{1,0:T(8,128)S(1)}, u32[]{:S(2)}, u32[]{:S(2)}) collective-permute-start(f32[64,128]{1,0:T(8,128)} %get-tuple-element.30), channel_id=1, source_target_pairs={{0,8},{8,16},{16,24},{24,0},{1,9},{9,17},{17,25},{25,1},{2,10},{10... | collective-permute-start | bytes 98312 | tf_op jit(solution)/shard_map/ppermute | solution.py:556
  32.3 6.6 %collective-permute-start.1 = (f32[64,128]{1,0:T(8,128)}, f32[64,128]{1,0:T(8,128)S(1)}, u32[]{:S(2)}, u32[]{:S(2)}) collective-permute-start(f32[64,128]{1,0:T(8,128)} %get-tuple-element.31), channel_id=1, source_target_pairs={{8,0},{16,8},{24,16},{0,24},{9,1},{17,9},{25,17},{1,25},{10,2},{18... | collective-permute-start | bytes 98312 | tf_op jit(solution)/shard_map/ppermute | solution.py:556
  38.9 0.6 copy-start.2
  39.5 0.6 copy-start.3
  42.1 10.8 %copy-start.11 = (f32[2,34,128]{2,1,0:T(8,128)S(1)}, f32[2,34,128]{2,1,0:T(8,128)}, u32[]{:S(2)}) copy-start(f32[2,34,128]{2,1,0:T(8,128)} %get-tuple-element.37) | copy-start | bytes 104452
  42.1 12.9 %copy-start.10 = (f32[2,34,128]{2,1,0:T(8,128)S(1)}, f32[2,34,128]{2,1,0:T(8,128)}, u32[]{:S(2)}) copy-start(f32[2,34,128]{2,1,0:T(8,128)} %get-tuple-element.38) | copy-start | bytes 104452
  42.1 19.2 %all-to-all-start.1 = ((f32[288,1,128]{2,1,0:T(1,128)}), f32[288,1,128]{2,1,0:T(1,128)S(1)}, u32[]{:S(2)}, u32[]{:S(2)}) async-start(f32[288,1,128]{2,1,0:T(1,128)} %get-tuple-element.35), calls=%async_computation.1 | async-start | bytes 294912 | tf_op jit(solution)/shard_map/all_to_all | solution.py:545
  52.9 4.1 %collective-permute-start.2 = (f32[2,34,128]{2,1,0:T(8,128)S(1)}, f32[2,34,128]{2,1,0:T(8,128)S(1)}, u32[]{:S(2)}, u32[]{:S(2)}) collective-permute-start(f32[2,34,128]{2,1,0:T(8,128)S(1)} %copy-done.11), channel_id=1, source_target_pairs={{0,1},{1,2},{2,3},{3,4},{4,5},{5,6},{6,7},{8,9},{9,10},{10,11},{11... | collective-permute-start | bytes 104456 | tf_op jit(solution)/shard_map/ppermute | solution.py:561
  55.0 4.2 %collective-permute-start.3 = (f32[2,34,128]{2,1,0:T(8,128)S(1)}, f32[2,34,128]{2,1,0:T(8,128)S(1)}, u32[]{:S(2)}, u32[]{:S(2)}) collective-permute-start(f32[2,34,128]{2,1,0:T(8,128)S(1)} %copy-done.10), channel_id=1, source_target_pairs={{1,0},{2,1},{3,2},{4,3},{5,4},{6,5},{7,6},{9,8},{10,9},{11,10},{12... | collective-permute-start | bytes 104456 | tf_op jit(solution)/shard_map/ppermute | solution.py:561
  57.0 4.3 %copy-start.4 = (f32[2,34,128]{2,1,0:T(8,128)}, f32[2,34,128]{2,1,0:T(8,128)S(1)}, u32[]{:S(2)}) copy-start(f32[2,34,128]{2,1,0:T(8,128)S(1)} %collective-permute-done.2.side_before) | copy-start | bytes 104452
  59.3 2.0 %copy-start.5 = (f32[2,34,128]{2,1,0:T(8,128)}, f32[2,34,128]{2,1,0:T(8,128)S(1)}, u32[]{:S(2)}) copy-start(f32[2,34,128]{2,1,0:T(8,128)S(1)} %collective-permute-done.3.side_after) | copy-start | bytes 104452
  61.3 0.6 copy-start
  68.6 14.2 %collective-permute-start.4 = (f32[32,128]{1,0:T(8,128)}, f32[32,128]{1,0:T(8,128)S(1)}, u32[]{:S(2)}, u32[]{:S(2)}) collective-permute-start(f32[32,128]{1,0:T(8,128)} %get-tuple-element.41), channel_id=1, source_target_pairs={{0,8},{8,16},{16,24},{24,0},{1,9},{9,17},{17,25},{25,1},{2,10},{10... | collective-permute-start | bytes 49160 | tf_op jit(solution)/shard_map/ppermute | solution.py:556
  70.2 12.6 %collective-permute-start.5 = (f32[32,128]{1,0:T(8,128)}, f32[32,128]{1,0:T(8,128)S(1)}, u32[]{:S(2)}, u32[]{:S(2)}) collective-permute-start(f32[32,128]{1,0:T(8,128)} %get-tuple-element.42), channel_id=1, source_target_pairs={{8,0},{16,8},{24,16},{0,24},{9,1},{17,9},{25,17},{1,25},{10,2},{18... | collective-permute-start | bytes 49160 | tf_op jit(solution)/shard_map/ppermute | solution.py:556
  72.5 10.3 %collective-permute-start.6 = (f32[32,128]{1,0:T(8,128)}, f32[32,128]{1,0:T(8,128)S(1)}, u32[]{:S(2)}, u32[]{:S(2)}) collective-permute-start(f32[32,128]{1,0:T(8,128)} %get-tuple-element.43), channel_id=1, source_target_pairs={{0,1},{1,2},{2,3},{3,4},{4,5},{5,6},{6,7},{8,9},{9,10},{10,11},{11... | collective-permute-start | bytes 49160 | tf_op jit(solution)/shard_map/ppermute | solution.py:561
  77.1 5.7 %collective-permute-start.7 = (f32[32,128]{1,0:T(8,128)}, f32[32,128]{1,0:T(8,128)S(1)}, u32[]{:S(2)}, u32[]{:S(2)}) collective-permute-start(f32[32,128]{1,0:T(8,128)} %get-tuple-element.44), channel_id=1, source_target_pairs={{1,0},{2,1},{3,2},{4,3},{5,4},{6,5},{7,6},{9,8},{10,9},{11,10},{12... | collective-permute-start | bytes 49160 | tf_op jit(solution)/shard_map/ppermute | solution.py:561
  82.8 0.6 copy-start.6
  82.8 0.6 copy-start.7
  82.8 0.6 copy-start.8
  82.8 0.6 copy-start.9
  86.2 21.2 %all-to-all-start.2 = ((f32[288,1,128]{2,1,0:T(1,128)}), f32[288,1,128]{2,1,0:T(1,128)S(1)}, u32[]{:S(2)}, u32[]{:S(2)}) async-start(f32[288,1,128]{2,1,0:T(1,128)} %last_smooth.1), calls=%async_computation.2 | async-start | bytes 294912 | tf_op jit(solution)/shard_map/all_to_all | solution.py:545
  107.4 0.6 copy-start.1
  110.8 0.7 copy-start.12
where the time goes:
time: 113 us; the launch traced here: 112 us
  starting transfers between devices  40.6 us (36%)
  Pallas kernels  34.1 us (30%)
  blocking collectives  18.2 us (16%)
  waiting for transfers between devices  12.7 us (11%)
  local copies, waits for them, and re-layouts  4.31 us (4%)
  between operations  1.43 us (1%)
    pallas_call x8, Pallas kernels, call(): pl.pallas_call(kernel, out_shape=outs, in_specs=list(ins), out_specs=out_...  34.1 us
    all_to_all x2, starting transfers between devices, exchange_all(): return lax.all_to_all(x, AXES, split_axis=0, concat_axis=0, tiled=True)  23.5 us
    all_to_all x1, blocking collectives, exchange_all(): return lax.all_to_all(x, AXES, split_axis=0, concat_axis=0, tiled=True)  18.2 us
    all_to_all x2, waiting for transfers between devices, exchange_all(): return lax.all_to_all(x, AXES, split_axis=0, concat_axis=0, tiled=True)  10.4 us
    ppermute x4, starting transfers between devices, lat_halo(): return (lax.ppermute(lb, 'lat', up), lax.ppermute(la, 'lat', down))  9.36 us
    ppermute x4, starting transfers between devices, lon_halo(): return (lax.ppermute(hi, 'lon', up), lax.ppermute(lo, 'lon', down))  7.75 us
    unnamed x26, local copies, waits for them, and re-layouts  3.79 us
    ppermute x4, waiting for transfers between devices, lat_halo(): return (lax.ppermute(lb, 'lat', up), lax.ppermute(la, 'lat', down))  2.3 us
  transfers between devices with their start and end apart: 10, of which 3 were waited for; matrix products, arithmetic and copies ran while one was open for 1% of the time, Pallas kernels for 8%

commit v1 on v0

--- a/solution.py
+++ b/solution.py
@@ -32,13 +32,23 @@
     return jax.ShapeDtypeStruct(shape, dtype)
 
 
-def call(kernel, outs, ins, args, scratch=(), out_specs=None, name=None):
+def near(shape, dtype=f32):
+    return pltpu.VMEM(shape, dtype)
+
+
+def call(kernel, outs, ins, args, scratch=(), out_specs=None, name=None, keep=True):
+    if keep:
+        args = [
+            pltpu.with_memory_space_constraint(x, pltpu.VMEM) if spec is VM else x
+            for x, spec in zip(args, ins)
+        ]
     return pl.pallas_call(
         kernel,
         out_shape=outs,
         in_specs=list(ins),
         out_specs=out_specs if out_specs is not None else [VM] * len(outs),
         scratch_shapes=list(scratch),
+        compiler_params=pltpu.CompilerParams(vmem_limit_bytes=20 << 20),
         name=name,
     )(*args)
 
@@ -571,24 +581,25 @@
     ray_rows = devices * rays // 128
     room = slots + CH
     flat = lambda x: x.reshape(tiles, segs)
-    layer_outs = [sds(s) for s in LAYERS]
-    grid = sds((COLS, DEP))
+    layer_outs = [near(s) for s in LAYERS]
+    grid = near((COLS, DEP))
     buf = lambda dtype: pltpu.VMEM((ROWS_M, ROWS_N), dtype)
 
     (packed,) = call(
         pack_kernel(devices, cap, rays, per_ray),
-        [sds((devices * width, 1, 128))],
+        [near((devices * width, 1, 128))],
         [SM, SM, SM, VM, VM, VM],
         (tile_brick.T, ray_counts, travel_times, flat(cell_offsets), flat(cell_depths), flat(seg_lengths)),
         [pltpu.VMEM((tiles, segs), f32)] * 2 + [pltpu.SMEM((devices,), i32)],
         name="pack",
+        keep=False,
     )
     recv0 = exchange_all(packed)
     chunks = room // CH + 1
-    grouped = sds((chunks * GROUPS, LANES))
+    grouped = near((chunks * GROUPS, LANES))
     g, lo, hi, gcell, gw, q, data, total, base, more = call(
         start_kernel(devices, cap, rays),
-        [grid, sds((2 * CLAT, DEP)), sds((2 * CLAT, DEP)), grouped, grouped, sds((room, 128)), sds((ray_rows, 128)),
+        [grid, near((2 * CLAT, DEP)), near((2 * CLAT, DEP)), grouped, grouped, near((room, 128)), near((ray_rows, 128)),
          sds((1,), i32), sds((chunks * GROUPS,), i32), sds((chunks,), i32)],
         [VM],
         (recv0,),
@@ -600,12 +611,12 @@
     tiles_of = (total, base, more)
     before, after = lon_halo(lo, hi)
     (y1,) = call(
-        forward_kernel(ray_rows), [sds((ray_rows, 128))], [SM] * 3 + [VM] * 4, (*tiles_of, g, gcell, gw, q),
+        forward_kernel(ray_rows), [near((ray_rows, 128))], [SM] * 3 + [VM] * 4, (*tiles_of, g, gcell, gw, q),
         gather_scratch, name="forward",
     )
     la, lb, send = call(
         edge_kernel(devices, ray_rows),
-        [sds(SIDE), sds(SIDE), sds((devices * (ray_rows + 1), 1, 128))],
+        [near(SIDE), near(SIDE), near((devices * (ray_rows + 1), 1, 128))],
         [VM] * 4,
         (g, before, after, y1),
         name="edge",
@@ -616,7 +627,7 @@
     place = jnp.stack([lat, lax.axis_size("lat") - 1 - lat]).astype(i32)
     z, lo, hi, la, lb, q1, p1, r2, num = call(
         second_kernel(devices, ray_rows),
-        [grid, *layer_outs, grid, sds((ray_rows, 128)), sds((ray_rows, 128)), sds((1, 128))],
+        [grid, *layer_outs, grid, near((ray_rows, 128)), near((ray_rows, 128)), near((1, 128))],
         [SM] * 4 + [VM] * 10,
         (*tiles_of, place, recv1, data, g, before, after, *sides, gcell, gw, q),
         [pltpu.VMEM((room, 128), f32), buf(f32)] + [pltpu.VMEM((CLAT, DEP), f32)] * 4,
@@ -624,12 +635,12 @@
     )
     around = lon_halo(lo, hi) + lat_halo(la, lb)
     (y2,) = call(
-        forward_kernel(ray_rows), [sds((ray_rows, 128))], [SM] * 3 + [VM] * 4, (*tiles_of, z, gcell, gw, q),
+        forward_kernel(ray_rows), [near((ray_rows, 128))], [SM] * 3 + [VM] * 4, (*tiles_of, z, gcell, gw, q),
         gather_scratch, name="forward",
     )
     (send,) = call(
         last_smooth_kernel(devices, ray_rows),
-        [sds((devices * (ray_rows + 1), 1, 128))],
+        [near((devices * (ray_rows + 1), 1, 128))],
         [VM] * 8,
         (z, g, q1, *around, y2),
         name="last_smooth",
@@ -638,7 +649,7 @@
     me = lax.axis_index(AXES).astype(i32).reshape(1)
     model, mis = call(
         final_kernel(devices, ray_rows, rays),
-        [grid, sds((1, 128))],
+        [sds((COLS, DEP)), sds((1, 128))],
         [SM] + [VM] * 7,
         (me, recv2, data, p1, r2, num, g, z),
         name="final",

time: 113 us -> 98.1 us (0.87); the launches traced: 112 us -> 98.6 us
  starting transfers between devices: 40.6 us -> 32.3 us
  Pallas kernels: 34.1 us -> 29.3 us
    all_to_all x2, starting transfers between devices: 23.5 us -> 15.9 us  [exchange_all(): return lax.all_to_all(x, AXES, split_axis=0, concat_axis=0, tiled=True)]
    pallas_call x8, Pallas kernels: 34.1 us -> 29.3 us  [call(): pl.pallas_call(kernel, out_shape=outs, in_specs=list(ins), out_specs=out_...]
    unnamed x26 -> x10, local copies, waits for them, and re-layouts: 3.79 us -> 3.19 us
  transfers between devices with their start and end apart: 10 -> 10, of which waited for: 3 -> 3; matrix products, arithmetic and copies ran while one was open for 1% -> 0% of each run, Pallas kernels for 8% -> 9%
where the time goes in v1:
time: 98.1 us; the launch traced here: 98.6 us
  starting transfers between devices  32.3 us (33%)
  Pallas kernels  29.3 us (30%)
  blocking collectives  18.6 us (19%)
  waiting for transfers between devices  13.3 us (14%)
  local copies, waits for them, and re-layouts  3.7 us (4%)
  between operations  1.45 us (1%)
    pallas_call x8, Pallas kernels, call(): pl.pallas_call(kernel, out_shape=outs, in_specs=list(ins), out_specs=out_...  29.3 us
    all_to_all x1, blocking collectives, exchange_all(): return lax.all_to_all(x, AXES, split_axis=0, concat_axis=0, tiled=True)  18.6 us
    all_to_all x2, starting transfers between devices, exchange_all(): return lax.all_to_all(x, AXES, split_axis=0, concat_axis=0, tiled=True)  15.9 us
    all_to_all x2, waiting for transfers between devices, exchange_all(): return lax.all_to_all(x, AXES, split_axis=0, concat_axis=0, tiled=True)  10.4 us
    ppermute x4, starting transfers between devices, lat_halo(): return (lax.ppermute(lb, 'lat', up), lax.ppermute(la, 'lat', down))  8.55 us
    ppermute x4, starting transfers between devices, lon_halo(): return (lax.ppermute(hi, 'lon', up), lax.ppermute(lo, 'lon', down))  7.75 us
    unnamed x10, local copies, waits for them, and re-layouts  3.19 us
    ppermute x4, waiting for transfers between devices, lat_halo(): return (lax.ppermute(lb, 'lat', up), lax.ppermute(la, 'lat', down))  2.88 us
  transfers between devices with their start and end apart: 10, of which 3 were waited for; matrix products, arithmetic and copies ran while one was open for 0% of the time, Pallas kernels for 9%

profile of v1, /device:TPU:0, one launch (start us, length us, event | category | flops | bytes accessed | tf_op | source)
XLA Modules:
  0.0 98.6 jit_solution(10140714040348696458)
XLA Ops:
  1.3 0.7 copy-done.3
  2.0 0.8 copy-done
  2.8 0.8 copy-done.1
  3.6 0.8 copy-done.2
  4.5 3.5 %pack.1 = f32[544,1,128]{2,1,0:T(1,128)S(1)} custom-call(s32[4,32]{1,0:T(4,128)S(1)} %bitcast.13, s32[1]{0:T(128)S(6)} %copy.8.counts, f32[32]{0:T(128)S(1)} %copy-done.4, s32[128,128]{1,0:T(8,128)S(1)} %bitcast.10, s32[128,128]{1,0:T(8,128)S(1)} %bitcast.11, f32[128,128]{1,0:T(8,128)S(1)} %bitcast.12), custom_call_target="tpu_custom_call" | custom-call | tf_op jit(solution)/shard_map/pack/pallas_call | solution.py:45
  8.0 18.6 %all_to_all.15.recv = f32[544,1,128]{2,1,0:T(1,128)S(1)} all-to-all(f32[544,1,128]{2,1,0:T(1,128)S(1)} %pack.1), channel_id=1, replica_groups=mesh['lon'=4,'lat'=8] {'lon','lat'}, dimensions={0} | all-to-all | bytes 557056 | tf_op jit(solution)/shard_map/all_to_all | solution.py:555
  26.5 6.6 %start.1 = (f32[1024,128]{1,0:T(8,128)S(1)}, f32[64,128]{1,0:T(8,128)S(1)}, f32[64,128]{1,0:T(8,128)S(1)}, f32[144,256]{1,0:T(8,128)S(1)}, f32[144,256]{1,0:T(8,...) custom-call(f32[544,1,128]{2,1,0:T(1,128)S(1)} %all_to_all.15.recv), custom_call_target="tpu_custom_call" | custom-call | tf_op jit(solution)/shard_map/start/pallas_call | solution.py:45
  33.2 1.0 %collective-permute-start = (f32[64,128]{1,0:T(8,128)S(1)}, f32[64,128]{1,0:T(8,128)S(1)}, u32[]{:S(2)}, u32[]{:S(2)}) collective-permute-start(f32[64,128]{1,0:T(8,128)S(1)} %get-tuple-element.30), channel_id=1, source_target_pairs={{0,8},{8,16},{16,24},{24,0},{1,9},{9,17},{17,25},{25,1},{2,10},{10... | collective-permute-start | bytes 98312 | tf_op jit(solution)/shard_map/ppermute | solution.py:566
  34.2 2.8 %collective-permute-start.1 = (f32[64,128]{1,0:T(8,128)S(1)}, f32[64,128]{1,0:T(8,128)S(1)}, u32[]{:S(2)}, u32[]{:S(2)}) collective-permute-start(f32[64,128]{1,0:T(8,128)S(1)} %get-tuple-element.31), channel_id=1, source_target_pairs={{8,0},{16,8},{24,16},{0,24},{9,1},{17,9},{25,17},{1,25},{10,2},{18... | collective-permute-start | bytes 98312 | tf_op jit(solution)/shard_map/ppermute | solution.py:566
  37.1 4.3 %forward.2.y = f32[8,128]{1,0:T(8,128)S(1)} custom-call(s32[1]{0:T(128)} %get-tuple-element.26.total, s32[144]{0:T(256)S(1)} %get-tuple-element.27.base, s32[18]{0:T(128)S(1)} %get-tuple-element.28.more, f32[1024,128]{1,0:T(8,128)S(1)} %get-tuple-element.29.src.g, f32[144,256]{1,0:T(8,128)S(1)} %get-tuple-element.32.gcell, ...), custom_call_target="tpu_custom_call" | custom-call | tf_op jit(solution)/shard_map/forward/pallas_call | solution.py:45
  41.4 0.0 collective-permute-done.before
  41.4 0.0 collective-permute-done.1.after
  41.4 0.9 edge.1
  42.4 6.8 %all-to-all-start.1 = ((f32[288,1,128]{2,1,0:T(1,128)}), f32[288,1,128]{2,1,0:T(1,128)S(1)}, u32[]{:S(2)}, u32[]{:S(2)}) async-start(f32[288,1,128]{2,1,0:T(1,128)} %get-tuple-element.35), calls=%async_computation.1 | async-start | bytes 294912 | tf_op jit(solution)/shard_map/all_to_all | solution.py:555
  49.1 2.2 %collective-permute-start.2 = (f32[2,34,128]{2,1,0:T(8,128)S(1)}, f32[2,34,128]{2,1,0:T(8,128)S(1)}, u32[]{:S(2)}, u32[]{:S(2)}) collective-permute-start(f32[2,34,128]{2,1,0:T(8,128)S(1)} %get-tuple-element.37), channel_id=1, source_target_pairs={{0,1},{1,2},{2,3},{3,4},{4,5},{5,6},{6,7},{8,9},{9,10},{10,11},{11... | collective-permute-start | bytes 104456 | tf_op jit(solution)/shard_map/ppermute | solution.py:571
  51.3 1.3 %collective-permute-start.3 = (f32[2,34,128]{2,1,0:T(8,128)S(1)}, f32[2,34,128]{2,1,0:T(8,128)S(1)}, u32[]{:S(2)}, u32[]{:S(2)}) collective-permute-start(f32[2,34,128]{2,1,0:T(8,128)S(1)} %get-tuple-element.38), channel_id=1, source_target_pairs={{1,0},{2,1},{3,2},{4,3},{5,4},{6,5},{7,6},{9,8},{10,9},{11,10},{12... | collective-permute-start | bytes 104456 | tf_op jit(solution)/shard_map/ppermute | solution.py:571
  52.6 0.1 pad_add_fusion.place
  52.7 0.0 collective-permute-done.2.side_before
  52.7 2.9 %collective-permute-done.3.side_after = f32[2,34,128]{2,1,0:T(8,128)S(1)} collective-permute-done((f32[2,34,128]{2,1,0:T(8,128)S(1)}, f32[2,34,128]{2,1,0:T(8,128)S(1)}, u32[]{:S(2)}, u32[]{:S(2)}) %collective-permute-start.3) | collective-permute-done | bytes 34848 | tf_op jit(solution)/shard_map/ppermute | solution.py:571
  55.6 2.0 %all-to-all-done.1.recv = f32[288,1,128]{2,1,0:T(1,128)S(1)} async-done(((f32[288,1,128]{2,1,0:T(1,128)}), f32[288,1,128]{2,1,0:T(1,128)S(1)}, u32[]{:S(2)}, u32[]{:S(2)}) %all-to-all-start.1) | async-done | bytes 147488 | tf_op jit(solution)/shard_map/all_to_all | solution.py:555
  57.5 6.7 %second.1 = (f32[1024,128]{1,0:T(8,128)S(1)}, f32[32,128]{1,0:T(8,128)S(1)}, f32[32,128]{1,0:T(8,128)S(1)}, f32[32,128]{1,0:T(8,128)S(1)}, f32[32,128]{1,0:T(8,1...) custom-call(s32[1]{0:T(128)} %get-tuple-element.26.total, ...), custom_call_target="tpu_custom_call" | custom-call | tf_op jit(solution)/shard_map/second/pallas_call | solution.py:45
  64.2 1.0 %collective-permute-start.4 = (f32[32,128]{1,0:T(8,128)S(1)}, f32[32,128]{1,0:T(8,128)S(1)}, u32[]{:S(2)}, u32[]{:S(2)}) collective-permute-start(f32[32,128]{1,0:T(8,128)S(1)} %get-tuple-element.41), channel_id=1, source_target_pairs={{0,8},{8,16},{16,24},{24,0},{1,9},{9,17},{17,25},{25,1},{2,10},{10... | collective-permute-start | bytes 49160 | tf_op jit(solution)/shard_map/ppermute | solution.py:566
  65.3 2.9 %collective-permute-start.5 = (f32[32,128]{1,0:T(8,128)S(1)}, f32[32,128]{1,0:T(8,128)S(1)}, u32[]{:S(2)}, u32[]{:S(2)}) collective-permute-start(f32[32,128]{1,0:T(8,128)S(1)} %get-tuple-element.42), channel_id=1, source_target_pairs={{8,0},{16,8},{24,16},{0,24},{9,1},{17,9},{25,17},{1,25},{10,2},{18... | collective-permute-start | bytes 49160 | tf_op jit(solution)/shard_map/ppermute | solution.py:566
  68.1 3.8 %collective-permute-start.6 = (f32[32,128]{1,0:T(8,128)S(1)}, f32[32,128]{1,0:T(8,128)S(1)}, u32[]{:S(2)}, u32[]{:S(2)}) collective-permute-start(f32[32,128]{1,0:T(8,128)S(1)} %get-tuple-element.43), channel_id=1, source_target_pairs={{0,1},{1,2},{2,3},{3,4},{4,5},{5,6},{6,7},{8,9},{9,10},{10,11},{11... | collective-permute-start | bytes 49160 | tf_op jit(solution)/shard_map/ppermute | solution.py:571
  71.9 1.3 %collective-permute-start.7 = (f32[32,128]{1,0:T(8,128)S(1)}, f32[32,128]{1,0:T(8,128)S(1)}, u32[]{:S(2)}, u32[]{:S(2)}) collective-permute-start(f32[32,128]{1,0:T(8,128)S(1)} %get-tuple-element.44), channel_id=1, source_target_pairs={{1,0},{2,1},{3,2},{4,3},{5,4},{6,5},{7,6},{9,8},{10,9},{11,10},{12... | collective-permute-start | bytes 49160 | tf_op jit(solution)/shard_map/ppermute | solution.py:571
  73.2 4.3 %forward.3.y = f32[8,128]{1,0:T(8,128)S(1)} custom-call(s32[1]{0:T(128)} %get-tuple-element.26.total, s32[144]{0:T(256)S(1)} %get-tuple-element.27.base, s32[18]{0:T(128)S(1)} %get-tuple-element.28.more, f32[1024,128]{1,0:T(8,128)S(1)} %get-tuple-element.39.src.z, f32[144,256]{1,0:T(8,128)S(1)} %get-tuple-element.32.gcell, ...), custom_call_target="tpu_custom_call" | custom-call | tf_op jit(solution)/shard_map/forward/pallas_call | solution.py:45
  77.6 0.0 collective-permute-done.4.before
  77.6 1.4 %last_smooth.1 = f32[288,1,128]{2,1,0:T(1,128)} custom-call(f32[1024,128]{1,0:T(8,128)S(1)} %get-tuple-element.39.src.z, f32[1024,128]{1,0:T(8,128)S(1)} %get-tuple-element.29.src.g, f32[1024,128]{1,0:T(8,128)S(1)} %get-tuple-element.40.q1, f32[32,128]{1,0:T(8,128)S(1)} %collective-permute-done.4.before, f32[32,128]{1,0:T(8,128)S(1)} %collective-permute-done.5.after, ...), custom_call_target="tpu_custom_call" | custom-call | tf_op jit(solution)/shard_map/last_smooth/pallas_call | solution.py:45
  79.0 9.2 %all-to-all-start.2 = ((f32[288,1,128]{2,1,0:T(1,128)}), f32[288,1,128]{2,1,0:T(1,128)S(1)}, u32[]{:S(2)}, u32[]{:S(2)}) async-start(f32[288,1,128]{2,1,0:T(1,128)} %last_smooth.1), calls=%async_computation.2 | async-start | bytes 294912 | tf_op jit(solution)/shard_map/all_to_all | solution.py:555
  88.2 8.4 %all-to-all-done.2.recv = f32[288,1,128]{2,1,0:T(1,128)S(1)} async-done(((f32[288,1,128]{2,1,0:T(1,128)}), f32[288,1,128]{2,1,0:T(1,128)S(1)}, u32[]{:S(2)}, u32[]{:S(2)}) %all-to-all-start.2) | async-done | bytes 147488 | tf_op jit(solution)/shard_map/all_to_all | solution.py:555
  96.6 1.5 %final.1 = (f32[1024,128]{1,0:T(8,128)}, f32[1,128]{1,0:T(1,128)S(1)}) custom-call(s32[1]{0:T(128)} %bitcast.me, f32[288,1,128]{2,1,0:T(1,128)S(1)} %all-to-all-done.2.recv, f32[8,128]{1,0:T(8,128)S(1)} %get-tuple-element.36.data_ref.data, f32[8,128]{1,0:T(8,128)S(1)} %get-tuple-element.45.p1, f32[8,128]{1,0:T(8,128)S(1)} %get-tuple-element.46.r2, ...), custom_call_target="tpu_custom_call" | custom-call | tf_op jit(solution)/shard_map/final/pallas_call | solution.py:45
  98.1 0.5 slice_bitcast_fusion
  (9 shorter events, 0.0 us)
Async XLA Ops:
  1.3 0.7 copy-start.3
  1.3 0.7 copy-start.4
  2.0 0.8 copy-start
  2.8 0.8 copy-start.1
  3.6 0.8 copy-start.2
  33.2 8.2 %collective-permute-start = (f32[64,128]{1,0:T(8,128)S(1)}, f32[64,128]{1,0:T(8,128)S(1)}, u32[]{:S(2)}, u32[]{:S(2)}) collective-permute-start(f32[64,128]{1,0:T(8,128)S(1)} %get-tuple-element.30), channel_id=1, source_target_pairs={{0,8},{8,16},{16,24},{24,0},{1,9},{9,17},{17,25},{25,1},{2,10},{10... | collective-permute-start | bytes 98312 | tf_op jit(solution)/shard_map/ppermute | solution.py:566
  34.2 7.2 %collective-permute-start.1 = (f32[64,128]{1,0:T(8,128)S(1)}, f32[64,128]{1,0:T(8,128)S(1)}, u32[]{:S(2)}, u32[]{:S(2)}) collective-permute-start(f32[64,128]{1,0:T(8,128)S(1)} %get-tuple-element.31), channel_id=1, source_target_pairs={{8,0},{16,8},{24,16},{0,24},{9,1},{17,9},{25,17},{1,25},{10,2},{18... | collective-permute-start | bytes 98312 | tf_op jit(solution)/shard_map/ppermute | solution.py:566
  42.4 15.2 %all-to-all-start.1 = ((f32[288,1,128]{2,1,0:T(1,128)}), f32[288,1,128]{2,1,0:T(1,128)S(1)}, u32[]{:S(2)}, u32[]{:S(2)}) async-start(f32[288,1,128]{2,1,0:T(1,128)} %get-tuple-element.35), calls=%async_computation.1 | async-start | bytes 294912 | tf_op jit(solution)/shard_map/all_to_all | solution.py:555
  49.1 3.5 %collective-permute-start.2 = (f32[2,34,128]{2,1,0:T(8,128)S(1)}, f32[2,34,128]{2,1,0:T(8,128)S(1)}, u32[]{:S(2)}, u32[]{:S(2)}) collective-permute-start(f32[2,34,128]{2,1,0:T(8,128)S(1)} %get-tuple-element.37), channel_id=1, source_target_pairs={{0,1},{1,2},{2,3},{3,4},{4,5},{5,6},{6,7},{8,9},{9,10},{10,11},{11... | collective-permute-start | bytes 104456 | tf_op jit(solution)/shard_map/ppermute | solution.py:571
  51.3 4.2 %collective-permute-start.3 = (f32[2,34,128]{2,1,0:T(8,128)S(1)}, f32[2,34,128]{2,1,0:T(8,128)S(1)}, u32[]{:S(2)}, u32[]{:S(2)}) collective-permute-start(f32[2,34,128]{2,1,0:T(8,128)S(1)} %get-tuple-element.38), channel_id=1, source_target_pairs={{1,0},{2,1},{3,2},{4,3},{5,4},{6,5},{7,6},{9,8},{10,9},{11,10},{12... | collective-permute-start | bytes 104456 | tf_op jit(solution)/shard_map/ppermute | solution.py:571
  64.2 13.3 %collective-permute-start.4 = (f32[32,128]{1,0:T(8,128)S(1)}, f32[32,128]{1,0:T(8,128)S(1)}, u32[]{:S(2)}, u32[]{:S(2)}) collective-permute-start(f32[32,128]{1,0:T(8,128)S(1)} %get-tuple-element.41), channel_id=1, source_target_pairs={{0,8},{8,16},{16,24},{24,0},{1,9},{9,17},{17,25},{25,1},{2,10},{10... | collective-permute-start | bytes 49160 | tf_op jit(solution)/shard_map/ppermute | solution.py:566
  65.3 12.3 %collective-permute-start.5 = (f32[32,128]{1,0:T(8,128)S(1)}, f32[32,128]{1,0:T(8,128)S(1)}, u32[]{:S(2)}, u32[]{:S(2)}) collective-permute-start(f32[32,128]{1,0:T(8,128)S(1)} %get-tuple-element.42), channel_id=1, source_target_pairs={{8,0},{16,8},{24,16},{0,24},{9,1},{17,9},{25,17},{1,25},{10,2},{18... | collective-permute-start | bytes 49160 | tf_op jit(solution)/shard_map/ppermute | solution.py:566
  68.1 9.5 %collective-permute-start.6 = (f32[32,128]{1,0:T(8,128)S(1)}, f32[32,128]{1,0:T(8,128)S(1)}, u32[]{:S(2)}, u32[]{:S(2)}) collective-permute-start(f32[32,128]{1,0:T(8,128)S(1)} %get-tuple-element.43), channel_id=1, source_target_pairs={{0,1},{1,2},{2,3},{3,4},{4,5},{5,6},{6,7},{8,9},{9,10},{10,11},{11... | collective-permute-start | bytes 49160 | tf_op jit(solution)/shard_map/ppermute | solution.py:571
  71.9 5.7 %collective-permute-start.7 = (f32[32,128]{1,0:T(8,128)S(1)}, f32[32,128]{1,0:T(8,128)S(1)}, u32[]{:S(2)}, u32[]{:S(2)}) collective-permute-start(f32[32,128]{1,0:T(8,128)S(1)} %get-tuple-element.44), channel_id=1, source_target_pairs={{1,0},{2,1},{3,2},{4,3},{5,4},{6,5},{7,6},{9,8},{10,9},{11,10},{12... | collective-permute-start | bytes 49160 | tf_op jit(solution)/shard_map/ppermute | solution.py:571
  79.0 17.6 %all-to-all-start.2 = ((f32[288,1,128]{2,1,0:T(1,128)}), f32[288,1,128]{2,1,0:T(1,128)S(1)}, u32[]{:S(2)}, u32[]{:S(2)}) async-start(f32[288,1,128]{2,1,0:T(1,128)} %last_smooth.1), calls=%async_computation.2 | async-start | bytes 294912 | tf_op jit(solution)/shard_map/all_to_all | solution.py:555
